TPU v7x, 32 devices: a whole 2x2x4 slice. The times are simulated.
32 devices in a mesh: com: 8 (over y, x, core), arc: 4 (over z).
Axes of the slice: x: 2, y: 2, z: 4, core: 2. Of those that a mesh axis runs over, the one named last changes fastest.
Arguments:
- flow_start: float32 [256, 65536], P('com', 'arc'), may hold values from 0 to 1
- price_start: float32 [256, 16384], P('com'), may hold values from -3 to 3
- cost: float32 [256, 65536], P('com', 'arc'), may hold values from -6 to 6
- demand: float32 [256, 16384], P('com'), may hold values from -6 to 6
- head_block: int32 [512], P('arc'), may hold values from 0 to 127
- tail_block: int32 [512], P('arc'), may hold values from 0 to 127
- head_local: int32 [65536], P('arc'), may hold values from 0 to 127
- tail_local: int32 [65536], P('arc'), may hold values from 0 to 127
- cap_class: int32 [65536], P('arc'), may hold values from 0 to 7
- cap_levels: float32 [8], replicated, may hold values from 25 to 128
Outputs:
- flow: float32 [256, 65536], P('com', 'arc')
- price: float32 [256, 16384], P('com')
Inputs may be any that keep to these rules, and one draw needn't show every extreme that they name: `head_block`: node block indices. `tail_block`: node block indices. `head_local`: positions within a node block. `tail_local`: positions within a node block.
All inputs are finite; a program needn't handle non-finite values.
Results may differ from a plain program's by a relative error of at most 0.00016.
Values sent between devices are 32-bit elements; how exact they have to be, the bound alone decides.
A program may use at most 128 MiB of HBM per device.

v0:
```python
import jax
import jax.numpy as jnp
from jax import lax
from jax.sharding import PartitionSpec as P

NODES = 16384
BLOCK = 128
CLASSES = 8
ITERS = 4
NEWTON = 3
step_primal = 0.25
step_dual = 0.1
soft_width = 0.05
highest = lax.Precision.HIGHEST


def column_sums(values, theta):
    excess = jnp.maximum(values - theta, 0.0)
    return (jnp.sum(excess, axis=0), jnp.sum(jnp.minimum(excess / soft_width, 1.0), axis=0))


def theta_step(theta, total, active, capacity):
    return theta + jnp.maximum(total - capacity, 0.0) / jnp.maximum(active, 1.0)


def on_device(
    flow_start,
    price_start,
    cost,
    demand,
    head_block,
    tail_block,
    head_local,
    tail_local,
    cap_class,
    cap_levels,
):
    com_rows, arc_cols = flow_start.shape
    blocks = arc_cols // BLOCK
    node_blocks = NODES // BLOCK
    lanes = jnp.arange(BLOCK, dtype=jnp.int32)
    head_table = (head_local.reshape(blocks, BLOCK)[:, :, None] == lanes).astype(jnp.float32)
    tail_table = (tail_local.reshape(blocks, BLOCK)[:, :, None] == lanes).astype(jnp.float32)
    block_ids = jnp.arange(node_blocks, dtype=jnp.int32)
    head_owner = (head_block[:, None] == block_ids).astype(jnp.float32)
    tail_owner = (tail_block[:, None] == block_ids).astype(jnp.float32)
    class_ids = jnp.arange(CLASSES, dtype=jnp.int32)
    capacity = jnp.sum(
        jnp.where(cap_class[:, None] == class_ids, cap_levels[None, :], 0.0), axis=1
    ).reshape(blocks, BLOCK)
    flow = flow_start.reshape(com_rows, blocks, BLOCK)
    unit_cost = cost.reshape(com_rows, blocks, BLOCK)
    price = price_start
    for step in range(ITERS):
        grid = price.reshape(com_rows, node_blocks, BLOCK)
        at_head = jnp.einsum("jn,knl->jkl", head_owner, grid, precision=highest)
        at_head = jnp.einsum("jkl,jal->kja", at_head, head_table, precision=highest)
        at_tail = jnp.einsum("jn,knl->jkl", tail_owner, grid, precision=highest)
        at_tail = jnp.einsum("jkl,jal->kja", at_tail, tail_table, precision=highest)
        trial = flow - step_primal * (unit_cost - (at_head - at_tail))
        values = lax.all_to_all(trial, "com", split_axis=1, concat_axis=0, tiled=True)
        limits = lax.all_to_all(capacity[None], "com", split_axis=1, concat_axis=0, tiled=True)
        theta = jnp.zeros(values.shape[1:], jnp.float32)
        for inner in range(NEWTON):
            total, active = column_sums(values, theta)
            theta = theta_step(theta, total, active, limits[0])
        fresh = lax.all_to_all(
            jnp.maximum(values - theta, 0.0), "com", split_axis=0, concat_axis=1, tiled=True
        )
        flows = 2.0 * fresh - flow
        inward = jnp.einsum("kja,jal->jkl", flows, head_table, precision=highest)
        inward = jnp.einsum("jn,jkl->knl", head_owner, inward, precision=highest)
        outward = jnp.einsum("kja,jal->jkl", flows, tail_table, precision=highest)
        outward = jnp.einsum("jn,jkl->knl", tail_owner, outward, precision=highest)
        balance = (inward - outward).reshape(com_rows, NODES)
        summed = lax.psum(balance, "arc")
        price = price + step_dual * (demand - summed)
        flow = fresh
    return (flow.reshape(com_rows, arc_cols), price)


def solution(mesh):
    return jax.shard_map(
        on_device,
        mesh=mesh,
        in_specs=(
            P("com", "arc"),
            P("com", None),
            P("com", "arc"),
            P("com", None),
            P("arc"),
            P("arc"),
            P("arc"),
            P("arc"),
            P("arc"),
            P(),
        ),
        out_specs=(P("com", "arc"), P("com", None)),
        check_vma=False,
    )
```

profile of v0, /device:TPU:0, one launch (start us, length us, event | category | flops | bytes accessed | tf_op | source)
XLA Modules:
  0.0 859.6 jit_solution(16881110937198093419)
XLA Ops:
  7.2 2.1 copy.138
  11.9 9.8 %fusion.7 = f32[128,128,32]{1,2,0:T(8,128)S(1)} fusion(s32[128,128]{1,0:T(8,128)S(1)} %bitcast.332, f32[128,32,128]{2,0,1:T(8,128)S(1)} %fusion.132), kind=kOutput, calls=%fused_computation.8 | convolution fusion | flops 807403520 | bytes 4259840 | tf_op jit(solution)/shard_map/jkl,jal->kja/dot_general | solution.py:59
  21.8 9.1 %fusion.33 = f32[32,128,128]{2,0,1:T(8,128)} fusion(f32[128,128,32]{1,2,0:T(8,128)S(1)} %fusion.7, f32[128,32,128]{2,0,1:T(8,128)S(1)} %fusion.119, s32[128,128]{1,0:T(8,128)S(1)} %bitcast.323, f32[32,16384]{1,0:T(8,128)S(1)} %copy-done, f32[32,16384]{1,0:T(8,128)S(1)} %copy-done.9), kind=kOutput, calls=%fused_computation.44 | convolution fusion | flops 809500672 | bytes 10551296 | tf_op jit(solution)/shard_map/jkl,jal->kja/dot_general | solution.py:57
  30.9 5.3 all-to-all-start
  37.1 25.8 %all-to-all-done = f32[32,128,128]{2,0,1:T(8,128)} async-done(((f32[32,128,128]{2,0,1:T(8,128)}), f32[32,128,128]{2,0,1:T(8,128)}, u32[]{:S(2)}, u32[]{:S(2)}) %all-to-all-start) | async-done | bytes 2097184 | tf_op jit(solution)/shard_map/all_to_all | solution.py:61
  62.9 3.4 all-to-all-start.1
  66.3 3.1 fusion.78
  69.4 4.1 copy.105
  73.5 3.2 fusion.82
  76.8 3.1 fusion.83
  80.1 30.6 %all_to_all.168 = f32[256,16,128]{2,1,0:T(8,128)S(1)} all-to-all(f32[256,16,128]{2,1,0:T(8,128)S(1)} %fusion.43), channel_id=1, replica_groups=mesh['com'=8,'arc'=4] {'com'}, dimensions={0} | all-to-all | bytes 4194304 | tf_op jit(solution)/shard_map/all_to_all | solution.py:67
  113.6 7.4 fusion.6
  121.0 7.5 fusion.14
  128.5 2.6 fusion.72
  131.1 4.0 subtract_bitcast_fusion.3
  135.1 2.9 copy.110
  138.0 4.1 copy.234
  142.5 86.0 %all-reduce.5.cloned.1.call-done = f32[32,16384]{1,0:T(8,128)} async-done(((f32[32,16384]{1,0:T(8,128)}), f32[32,16384]{1,0:T(8,128)}) %all-reduce.5.cloned.1.call-update) | async-done | bytes 2097168 | tf_op jit(solution)/shard_map/psum | solution.py:76
  228.4 3.1 fusion.106
  234.5 9.8 %fusion.5 = f32[128,128,32]{1,2,0:T(8,128)S(1)} fusion(s32[128,128]{1,0:T(8,128)S(1)} %bitcast.334, f32[128,32,128]{2,0,1:T(8,128)S(1)} %fusion.129), kind=kOutput, calls=%fused_computation.6 | convolution fusion | flops 807403520 | bytes 4259840 | tf_op jit(solution)/shard_map/jkl,jal->kja/dot_general | solution.py:59
  244.3 10.2 %fusion.35 = f32[32,128,128]{2,0,1:T(8,128)S(1)} fusion(f32[32,8,16,128]{3,0,2,1:T(8,128)S(1)} %copy-done.6, f32[128,128,32]{1,2,0:T(8,128)S(1)} %fusion.5, f32[128,32,128]{2,0,1:T(8,128)S(1)} %fusion.116, s32[128,128]{1,0:T(8,128)S(1)} %bitcast.325, f32[32,16384]{1,0:T(8,128)S(1)} %copy-done), kind=kOutput, calls=%fused_computation.46 | convolution fusion | flops 809500672 | bytes 10551296 | tf_op jit(solution)/shard_map/jkl,jal->kja/dot_general | solution.py:57
  254.5 30.0 %all_to_all.169 = f32[32,128,128]{2,0,1:T(8,128)S(1)} all-to-all(f32[32,128,128]{2,0,1:T(8,128)S(1)} %fusion.35), channel_id=1, replica_groups=mesh['com'=8,'arc'=4] {'com'}, dimensions={1} | all-to-all | bytes 4194304 | tf_op jit(solution)/shard_map/all_to_all | solution.py:61
  284.5 1.6 fusion.79
  287.4 1.6 fusion.84
  289.0 1.6 fusion.85
  290.8 29.4 %all_to_all.170 = f32[256,16,128]{2,1,0:T(8,128)S(1)} all-to-all(f32[256,16,128]{2,1,0:T(8,128)S(1)} %fusion.42), channel_id=1, replica_groups=mesh['com'=8,'arc'=4] {'com'}, dimensions={0} | all-to-all | bytes 4194304 | tf_op jit(solution)/shard_map/all_to_all | solution.py:67
  322.2 7.4 fusion.4
  329.6 7.5 fusion.12
  337.1 2.6 fusion.66
  339.7 4.0 subtract_bitcast_fusion.2
  343.7 2.9 copy.118
  346.6 4.1 copy.233
  351.0 83.3 %all-reduce.7.cloned.1.call-done = f32[32,16384]{1,0:T(8,128)} async-done(((f32[32,16384]{1,0:T(8,128)}), f32[32,16384]{1,0:T(8,128)}) %all-reduce.7.cloned.1.call-update) | async-done | bytes 2097168 | tf_op jit(solution)/shard_map/psum | solution.py:76
  434.3 3.9 multiply_add_fusion.2
  442.1 9.8 %fusion.3 = f32[128,128,32]{1,2,0:T(8,128)S(1)} fusion(s32[128,128]{1,0:T(8,128)S(1)} %bitcast.336, f32[128,32,128]{2,0,1:T(8,128)S(1)} %fusion.126), kind=kOutput, calls=%fused_computation.4 | convolution fusion | flops 807403520 | bytes 4259840 | tf_op jit(solution)/shard_map/jkl,jal->kja/dot_general | solution.py:59
  451.9 10.2 %fusion.37 = f32[32,128,128]{2,0,1:T(8,128)S(1)} fusion(f32[32,8,16,128]{3,0,2,1:T(8,128)S(1)} %copy-done.4, f32[128,128,32]{1,2,0:T(8,128)S(1)} %fusion.3, f32[128,32,128]{2,0,1:T(8,128)S(1)} %fusion.113, s32[128,128]{1,0:T(8,128)S(1)} %bitcast.327, f32[32,16384]{1,0:T(8,128)S(1)} %copy-done), kind=kOutput, calls=%fused_computation.48 | convolution fusion | flops 809500672 | bytes 10551296 | tf_op jit(solution)/shard_map/jkl,jal->kja/dot_general | solution.py:57
  462.1 30.0 %all_to_all.171 = f32[32,128,128]{2,0,1:T(8,128)S(1)} all-to-all(f32[32,128,128]{2,0,1:T(8,128)S(1)} %fusion.37), channel_id=1, replica_groups=mesh['com'=8,'arc'=4] {'com'}, dimensions={1} | all-to-all | bytes 4194304 | tf_op jit(solution)/shard_map/all_to_all | solution.py:61
  495.0 1.6 fusion.86
  496.6 1.6 fusion.87
  498.4 29.2 %all_to_all.172 = f32[256,16,128]{2,1,0:T(8,128)S(1)} all-to-all(f32[256,16,128]{2,1,0:T(8,128)S(1)} %fusion.41), channel_id=1, replica_groups=mesh['com'=8,'arc'=4] {'com'}, dimensions={0} | all-to-all | bytes 4194304 | tf_op jit(solution)/shard_map/all_to_all | solution.py:67
  529.6 7.4 fusion.2
  537.0 7.5 fusion.10
  544.5 2.6 fusion.60
  547.1 4.0 subtract_bitcast_fusion.1
  551.1 2.9 copy.126
  554.0 4.1 copy.232
  558.6 83.1 %all-reduce.9.cloned.1.call-done = f32[32,16384]{1,0:T(8,128)} async-done(((f32[32,16384]{1,0:T(8,128)}), f32[32,16384]{1,0:T(8,128)}) %all-reduce.9.cloned.1.call-update) | async-done | bytes 2097168 | tf_op jit(solution)/shard_map/psum | solution.py:76
  641.7 3.1 fusion.107
  647.7 9.8 %fusion.1 = f32[128,128,32]{1,2,0:T(8,128)S(1)} fusion(s32[128,128]{1,0:T(8,128)S(1)} %bitcast.338, f32[128,32,128]{2,0,1:T(8,128)S(1)} %fusion.123), kind=kOutput, calls=%fused_computation.2 | convolution fusion | flops 807403520 | bytes 4259840 | tf_op jit(solution)/shard_map/jkl,jal->kja/dot_general | solution.py:59
  657.6 10.2 %fusion.39 = f32[32,128,128]{2,0,1:T(8,128)S(1)} fusion(f32[32,8,16,128]{3,0,2,1:T(8,128)S(1)} %copy-done.2, f32[128,128,32]{1,2,0:T(8,128)S(1)} %fusion.1, f32[128,32,128]{2,0,1:T(8,128)S(1)} %fusion.110, s32[128,128]{1,0:T(8,128)S(1)} %bitcast.329, f32[32,16384]{1,0:T(8,128)S(1)} %copy-done), kind=kOutput, calls=%fused_computation.50 | convolution fusion | flops 809500672 | bytes 10551296 | tf_op jit(solution)/shard_map/jkl,jal->kja/dot_general | solution.py:57
  667.8 30.0 %all_to_all.173 = f32[32,128,128]{2,0,1:T(8,128)S(1)} all-to-all(f32[32,128,128]{2,0,1:T(8,128)S(1)} %fusion.39), channel_id=1, replica_groups=mesh['com'=8,'arc'=4] {'com'}, dimensions={1} | all-to-all | bytes 4194304 | tf_op jit(solution)/shard_map/all_to_all | solution.py:61
  700.6 1.6 fusion.88
  702.3 1.6 fusion.89
  704.1 29.2 %all_to_all.174 = f32[256,16,128]{2,1,0:T(8,128)S(1)} all-to-all(f32[256,16,128]{2,1,0:T(8,128)S(1)} %fusion.40), channel_id=1, replica_groups=mesh['com'=8,'arc'=4] {'com'}, dimensions={0} | all-to-all | bytes 4194304 | tf_op jit(solution)/shard_map/all_to_all | solution.py:67
  735.5 7.5 fusion
  743.0 7.5 fusion.8
  750.5 2.6 fusion.54
  753.1 4.0 subtract_bitcast_fusion
  757.1 2.9 copy.135
  760.0 4.2 copy.230
  764.2 1.8 copy.131
  766.0 2.5 copy.231
  768.5 79.2 %all-reduce.11.cloned.1.call-done = f32[32,16384]{1,0:T(8,128)} async-done(((f32[32,16384]{1,0:T(8,128)}), f32[32,16384]{1,0:T(8,128)}) %all-reduce.11.cloned.1.call-update) | async-done | bytes 2097168 | tf_op jit(solution)/shard_map/psum | solution.py:76
  847.7 5.2 multiply_add_fusion
  (87 shorter events, 30.6 us)
Async XLA Ops:
  7.2 14.6 %copy-start = (f32[32,16384]{1,0:T(8,128)S(1)}, f32[32,16384]{1,0:T(8,128)}, u32[]{:S(2)}) copy-start(f32[32,16384]{1,0:T(8,128)} %param.12) | copy-start | bytes 6291460
  7.2 2.1 copy-start.15
  9.3 1.3 copy-start.16
  10.6 1.3 copy-start.13
  11.9 9.9 %copy-start.9 = (f32[32,16384]{1,0:T(8,128)S(1)}, f32[32,16384]{1,0:T(8,128)}, u32[]{:S(2)}) copy-start(f32[32,16384]{1,0:T(8,128)} %param.10) | copy-start | bytes 6291460
  11.9 9.9 %copy-start.12 = (s32[16384]{0:T(1024)S(1)}, s32[16384]{0:T(1024)}, u32[]{:S(2)}) copy-start(s32[16384]{0:T(1024)} %param.16) | copy-start | bytes 196612
  30.9 5.3 copy-start.14
  30.9 5.3 copy-start.17
  30.9 32.0 %all-to-all-start = ((f32[32,128,128]{2,0,1:T(8,128)}), f32[32,128,128]{2,0,1:T(8,128)}, u32[]{:S(2)}, u32[]{:S(2)}) async-start(f32[32,128,128]{2,0,1:T(8,128)} %fusion.33), calls=%async_computation | async-start | bytes 4194304 | tf_op jit(solution)/shard_map/all_to_all | solution.py:61
  62.9 10.6 %all-to-all-start.1 = ((f32[1,128,128]{2,0,1:T(1,128)}), f32[1,128,128]{2,0,1:T(1,128)S(1)}, u32[]{:S(2)}, u32[]{:S(2)}) async-start(f32[1,128,128]{2,0,1:T(1,128)} %bitcast.8), calls=%async_computation.1 | async-start | bytes 131072 | tf_op jit(solution)/shard_map/all_to_all | solution.py:62
  66.3 162.1 %all-reduce.5.cloned.1.call-start = ((), (), s32[]{:S(2)}) async-start(), calls=%async_computation.9 | async-start | bytes 4194304 | tf_op jit(solution)/shard_map/psum | solution.py:76
  73.5 6.4 copy-start.11
  110.7 1.6 copy-start.10
  112.3 1.3 copy-start.5
  142.2 292.1 %all-reduce.7.cloned.1.call-start = ((), (), s32[]{:S(2)}) async-start(), calls=%async_computation.10 | async-start | bytes 4194304 | tf_op jit(solution)/shard_map/psum | solution.py:76
  234.5 9.9 %copy-start.6 = (f32[32,8,16,128]{3,0,2,1:T(8,128)S(1)}, f32[32,8,16,128]{3,0,2,1:T(8,128)}, u32[]{:S(2)}) copy-start(f32[32,8,16,128]{3,0,2,1:T(8,128)} %copy-done.5) | copy-start | bytes 6291460
  320.9 1.3 copy-start.3
  350.7 290.9 %all-reduce.9.cloned.1.call-start = ((), (), s32[]{:S(2)}) async-start(), calls=%async_computation.11 | async-start | bytes 4194304 | tf_op jit(solution)/shard_map/psum | solution.py:76
  438.2 1.4 copy-start.7
  442.1 9.9 %copy-start.4 = (f32[32,8,16,128]{3,0,2,1:T(8,128)S(1)}, f32[32,8,16,128]{3,0,2,1:T(8,128)}, u32[]{:S(2)}) copy-start(f32[32,8,16,128]{3,0,2,1:T(8,128)} %copy-done.3) | copy-start | bytes 6291460
  528.3 1.3 copy-start.1
  558.1 289.5 %all-reduce.11.cloned.1.call-start = ((), (), s32[]{:S(2)}) async-start(), calls=%async_computation.12 | async-start | bytes 4194304 | tf_op jit(solution)/shard_map/psum | solution.py:76
  647.7 9.9 %copy-start.2 = (f32[32,8,16,128]{3,0,2,1:T(8,128)S(1)}, f32[32,8,16,128]{3,0,2,1:T(8,128)}, u32[]{:S(2)}) copy-start(f32[32,8,16,128]{3,0,2,1:T(8,128)} %copy-done.1) | copy-start | bytes 6291460
  733.3 1.3 copy-start.8
Sparse Core Ops, SparseCore 0:
  142.3 86.0 all-reduce.4
  350.9 83.3 all-reduce.6
  558.3 83.3 all-reduce.8
  764.3 83.3 all-reduce.10
where the time goes:
time: 868 us; the launch traced here: 860 us
  waiting for transfers between devices  357 us (41%)
  blocking collectives  209 us (24%)
  matrix products  175 us (20%)
  local copies, waits for them, and re-layouts  51.7 us (6%)
  other arithmetic  42.8 us (5%)
  between operations  14.6 us (2%)
  starting transfers between devices  9.63 us (1%)
    psum x4, waiting for transfers between devices, on_device(): summed = lax.psum(balance, 'arc')  332 us
    all_to_all x4, blocking collectives, on_device(): lax.all_to_all(jnp.maximum(values - theta, 0.0), 'com', split_axis=0, con...  118 us
    all_to_all x3, blocking collectives, on_device(): lax.all_to_all(trial, 'com', split_axis=1, concat_axis=0, tiled=True)  90 us
    dot_general x4, matrix products, on_device(): at_head = jnp.einsum('jkl,jal->kja', at_head, head_table, precision=highest)  39.7 us
    dot_general x4, matrix products, on_device(): at_tail = jnp.einsum('jkl,jal->kja', at_tail, tail_table, precision=highest)  39.3 us
    dot_general x4, matrix products, on_device(): inward = jnp.einsum('kja,jal->jkl', flows, head_table, precision=highest)  29.9 us
    dot_general x4, matrix products, on_device(): outward = jnp.einsum('kja,jal->jkl', flows, tail_table, precision=highest)  29.7 us
    unnamed x45, local copies, waits for them, and re-layouts  28 us
  transfers between devices with their start and end apart: 6, of which 5 were waited for; matrix products, arithmetic and copies ran while one was open for 1% of the time, Pallas kernels for 0%

commit v1 on v0

--- a/solution.py
+++ b/solution.py
@@ -73,7 +73,9 @@
         outward = jnp.einsum("kja,jal->jkl", flows, tail_table, precision=highest)
         outward = jnp.einsum("jn,jkl->knl", tail_owner, outward, precision=highest)
         balance = (inward - outward).reshape(com_rows, NODES)
-        summed = lax.psum(balance, "arc")
+        summed = balance
+        for hop in (1, 2):
+            summed = summed + lax.ppermute(summed, "arc", [(dev, dev ^ hop) for dev in range(4)])
         price = price + step_dual * (demand - summed)
         flow = fresh
     return (flow.reshape(com_rows, arc_cols), price)

time: 868 us -> 1060 us (1.22)
  waiting for transfers between devices: 357 us -> 565 us
  between operations: 14.6 us -> 1.69 us
  starting transfers between devices: 9.63 us -> 22.3 us
    ppermute x0 -> x8, waiting for transfers between devices: none -> 539 us  [on_device(): lax.ppermute(summed, 'arc', [(dev, dev ^ hop) for dev in range(4)])]
    psum x4 -> x0, waiting for transfers between devices: 332 us -> none  [on_device(): summed = lax.psum(balance, 'arc')]
    ppermute x0 -> x8, starting transfers between devices: none -> 13.6 us  [on_device(): lax.ppermute(summed, 'arc', [(dev, dev ^ hop) for dev in range(4)])]
    unnamed x45 -> x81, local copies, waits for them, and re-layouts: 28 us -> 25.2 us
  transfers between devices with their start and end apart: 6 -> 10, of which waited for: 5 -> 9; matrix products, arithmetic and copies ran while one was open for 1% -> 1% of each run, Pallas kernels for 0% -> 0%
where the time goes in v1:
time: 1060 us
  waiting for transfers between devices  565 us (53%)
  blocking collectives  208 us (20%)
  matrix products  175 us (17%)
  local copies, waits for them, and re-layouts  48.3 us (5%)
  other arithmetic  35.7 us (3%)
  starting transfers between devices  22.3 us (2%)
    ppermute x8, waiting for transfers between devices, on_device(): lax.ppermute(summed, 'arc', [(dev, dev ^ hop) for dev in range(4)])  539 us
    all_to_all x4, blocking collectives, on_device(): lax.all_to_all(jnp.maximum(values - theta, 0.0), 'com', split_axis=0, con...  119 us
    all_to_all x3, blocking collectives, on_device(): lax.all_to_all(trial, 'com', split_axis=1, concat_axis=0, tiled=True)  89.1 us
    dot_general x4, matrix products, on_device(): at_head = jnp.einsum('jkl,jal->kja', at_head, head_table, precision=highest)  39.7 us
    dot_general x4, matrix products, on_device(): at_tail = jnp.einsum('jkl,jal->kja', at_tail, tail_table, precision=highest)  39.3 us
    dot_general x4, matrix products, on_device(): inward = jnp.einsum('kja,jal->jkl', flows, head_table, precision=highest)  29.9 us
    dot_general x4, matrix products, on_device(): outward = jnp.einsum('kja,jal->jkl', flows, tail_table, precision=highest)  29.7 us
    all_to_all x1, waiting for transfers between devices, on_device(): lax.all_to_all(trial, 'com', split_axis=1, concat_axis=0, tiled=True)  25.8 us
  transfers between devices with their start and end apart: 10, of which 9 were waited for; matrix products, arithmetic and copies ran while one was open for 1% of the time, Pallas kernels for 0%

profile of v1, /device:TPU:0, one launch (start us, length us, event | category | flops | bytes accessed | tf_op | source)
XLA Modules:
  0.0 1055.7 jit_solution(3856493780195843177)
XLA Ops:
  0.7 2.1 copy.138
  5.4 9.8 fusion.7
  15.3 9.1 fusion.33
  24.3 5.3 all-to-all-start
  30.6 25.8 %all-to-all-done = f32[32,128,128]{2,0,1:T(8,128)} async-done(((f32[32,128,128]{2,0,1:T(8,128)}), f32[32,128,128]{2,0,1:T(8,128)}, u32[]{:S(2)}, u32[]{:S(2)}) %all-to-all-start) | async-done | bytes 2097184 | tf_op jit(solution)/shard_map/all_to_all | solution.py:61
  56.4 3.4 all-to-all-start.1
  59.7 3.1 fusion.78
  62.8 4.1 copy.105
  67.0 3.2 fusion.82
  70.2 3.1 fusion.83
  73.5 30.7 %all_to_all.168 = f32[256,16,128]{2,1,0:T(8,128)S(1)} all-to-all(f32[256,16,128]{2,1,0:T(8,128)S(1)} %fusion.43), channel_id=1, replica_groups=mesh['com'=8,'arc'=4] {'com'}, dimensions={0} | all-to-all | bytes 4194304 | tf_op jit(solution)/shard_map/all_to_all | solution.py:67
  107.1 7.4 fusion.6
  114.5 7.5 fusion.14
  122.0 2.6 fusion.72
  124.6 4.0 subtract_bitcast_fusion.3
  128.6 3.1 copy.110
  131.7 3.0 copy.242
  134.7 2.2 collective-permute-start
  136.9 45.1 %collective-permute-done = f32[32,16384]{1,0:T(8,128)S(1)} collective-permute-done((f32[32,16384]{1,0:T(8,128)S(1)}, f32[32,16384]{1,0:T(8,128)S(1)}, u32[]{:S(2)}, u32[]{:S(2)}) %collective-permute-start) | collective-permute-done | bytes 2097184 | tf_op jit(solution)/shard_map/ppermute | solution.py:78
  183.3 2.8 collective-permute-start.1
  186.1 89.3 %collective-permute-done.1 = f32[32,16384]{1,0:T(8,128)S(1)} collective-permute-done((f32[32,16384]{1,0:T(8,128)S(1)}, f32[32,16384]{1,0:T(8,128)S(1)}, u32[]{:S(2)}, u32[]{:S(2)}) %collective-permute-start.1) | collective-permute-done | bytes 2097184 | tf_op jit(solution)/shard_map/ppermute | solution.py:78
  279.7 9.8 fusion.5
  289.5 10.2 fusion.35
  299.7 29.7 %all_to_all.169 = f32[32,128,128]{2,0,1:T(8,128)S(1)} all-to-all(f32[32,128,128]{2,0,1:T(8,128)S(1)} %fusion.35), channel_id=1, replica_groups=mesh['com'=8,'arc'=4] {'com'}, dimensions={1} | all-to-all | bytes 4194304 | tf_op jit(solution)/shard_map/all_to_all | solution.py:61
  335.7 29.3 %all_to_all.170 = f32[256,16,128]{2,1,0:T(8,128)S(1)} all-to-all(f32[256,16,128]{2,1,0:T(8,128)S(1)} %fusion.42), channel_id=1, replica_groups=mesh['com'=8,'arc'=4] {'com'}, dimensions={0} | all-to-all | bytes 4194304 | tf_op jit(solution)/shard_map/all_to_all | solution.py:67
  367.0 7.4 fusion.4
  374.4 7.5 fusion.12
  381.9 2.6 fusion.66
  384.5 4.0 subtract_bitcast_fusion.2
  388.5 3.4 copy.118
  391.9 3.0 copy.241
  395.5 46.2 %collective-permute-done.2 = f32[32,16384]{1,0:T(8,128)S(1)} collective-permute-done((f32[32,16384]{1,0:T(8,128)S(1)}, f32[32,16384]{1,0:T(8,128)S(1)}, u32[]{:S(2)}, u32[]{:S(2)}) %collective-permute-start.2) | collective-permute-done | bytes 2097184 | tf_op jit(solution)/shard_map/ppermute | solution.py:78
  443.0 2.3 collective-permute-start.3
  445.3 89.6 %collective-permute-done.3 = f32[32,16384]{1,0:T(8,128)S(1)} collective-permute-done((f32[32,16384]{1,0:T(8,128)S(1)}, f32[32,16384]{1,0:T(8,128)S(1)}, u32[]{:S(2)}, u32[]{:S(2)}) %collective-permute-start.3) | collective-permute-done | bytes 2097184 | tf_op jit(solution)/shard_map/ppermute | solution.py:78
  539.1 9.8 fusion.3
  548.9 10.2 fusion.37
  559.1 29.6 %all_to_all.171 = f32[32,128,128]{2,0,1:T(8,128)S(1)} all-to-all(f32[32,128,128]{2,0,1:T(8,128)S(1)} %fusion.37), channel_id=1, replica_groups=mesh['com'=8,'arc'=4] {'com'}, dimensions={1} | all-to-all | bytes 4194304 | tf_op jit(solution)/shard_map/all_to_all | solution.py:61
  591.6 1.6 fusion.86
  595.0 29.2 %all_to_all.172 = f32[256,16,128]{2,1,0:T(8,128)S(1)} all-to-all(f32[256,16,128]{2,1,0:T(8,128)S(1)} %fusion.41), channel_id=1, replica_groups=mesh['com'=8,'arc'=4] {'com'}, dimensions={0} | all-to-all | bytes 4194304 | tf_op jit(solution)/shard_map/all_to_all | solution.py:67
  626.2 7.4 fusion.2
  633.6 7.5 fusion.10
  641.1 2.6 fusion.60
  643.8 4.0 subtract_bitcast_fusion.1
  647.7 3.1 copy.126
  650.9 3.0 copy.240
  654.5 46.2 %collective-permute-done.4 = f32[32,16384]{1,0:T(8,128)S(1)} collective-permute-done((f32[32,16384]{1,0:T(8,128)S(1)}, f32[32,16384]{1,0:T(8,128)S(1)}, u32[]{:S(2)}, u32[]{:S(2)}) %collective-permute-start.4) | collective-permute-done | bytes 2097184 | tf_op jit(solution)/shard_map/ppermute | solution.py:78
  702.1 2.3 collective-permute-start.5
  704.3 89.6 %collective-permute-done.5 = f32[32,16384]{1,0:T(8,128)S(1)} collective-permute-done((f32[32,16384]{1,0:T(8,128)S(1)}, f32[32,16384]{1,0:T(8,128)S(1)}, u32[]{:S(2)}, u32[]{:S(2)}) %collective-permute-start.5) | collective-permute-done | bytes 2097184 | tf_op jit(solution)/shard_map/ppermute | solution.py:78
  798.4 9.8 fusion.1
  808.3 10.2 fusion.39
  818.5 29.7 %all_to_all.173 = f32[32,128,128]{2,0,1:T(8,128)S(1)} all-to-all(f32[32,128,128]{2,0,1:T(8,128)S(1)} %fusion.39), channel_id=1, replica_groups=mesh['com'=8,'arc'=4] {'com'}, dimensions={1} | all-to-all | bytes 4194304 | tf_op jit(solution)/shard_map/all_to_all | solution.py:61
  851.1 1.6 fusion.88
  854.5 29.5 %all_to_all.174 = f32[256,16,128]{2,1,0:T(8,128)S(1)} all-to-all(f32[256,16,128]{2,1,0:T(8,128)S(1)} %fusion.40), channel_id=1, replica_groups=mesh['com'=8,'arc'=4] {'com'}, dimensions={0} | all-to-all | bytes 4194304 | tf_op jit(solution)/shard_map/all_to_all | solution.py:67
  886.3 7.5 fusion
  893.7 7.5 fusion.8
  901.2 2.6 fusion.54
  903.9 4.0 subtract_bitcast_fusion
  907.8 3.0 copy.135
  910.9 3.0 copy.238
  914.5 46.2 %collective-permute-done.6 = f32[32,16384]{1,0:T(8,128)S(1)} collective-permute-done((f32[32,16384]{1,0:T(8,128)S(1)}, f32[32,16384]{1,0:T(8,128)S(1)}, u32[]{:S(2)}, u32[]{:S(2)}) %collective-permute-start.6) | collective-permute-done | bytes 2097184 | tf_op jit(solution)/shard_map/ppermute | solution.py:78
  962.0 2.3 collective-permute-start.7
  964.5 2.5 copy.239
  967.0 86.8 %collective-permute-done.7 = f32[32,16384]{1,0:T(8,128)S(1)} collective-permute-done((f32[32,16384]{1,0:T(8,128)S(1)}, f32[32,16384]{1,0:T(8,128)S(1)}, u32[]{:S(2)}, u32[]{:S(2)}) %collective-permute-start.7) | collective-permute-done | bytes 2097184 | tf_op jit(solution)/shard_map/ppermute | solution.py:78
  1053.8 1.7 multiply_add_fusion
  (131 shorter events, 48.3 us)
Async XLA Ops:
  0.6 14.6 %copy-start = (f32[32,16384]{1,0:T(8,128)S(1)}, f32[32,16384]{1,0:T(8,128)}, u32[]{:S(2)}) copy-start(f32[32,16384]{1,0:T(8,128)} %param.12) | copy-start | bytes 6291460
  0.6 2.1 copy-start.33
  2.8 1.3 copy-start.34
  4.1 1.3 copy-start.31
  5.4 9.9 copy-start.24
  5.4 9.9 copy-start.30
  24.3 5.3 copy-start.32
  24.3 5.3 copy-start.35
  24.3 32.1 %all-to-all-start = ((f32[32,128,128]{2,0,1:T(8,128)}), f32[32,128,128]{2,0,1:T(8,128)}, u32[]{:S(2)}, u32[]{:S(2)}) async-start(f32[32,128,128]{2,0,1:T(8,128)} %fusion.33), calls=%async_computation | async-start | bytes 4194304 | tf_op jit(solution)/shard_map/all_to_all | solution.py:61
  56.4 10.6 all-to-all-start.1
  66.9 6.4 copy-start.29
  104.2 1.6 copy-start.25
  105.8 1.3 copy-start.10
  131.7 50.2 %copy-start.18 = (f32[32,128,128]{2,1,0:T(8,128)S(1)}, f32[32,128,128]{2,1,0:T(8,128)}, u32[]{:S(2)}) copy-start(f32[32,128,128]{2,1,0:T(8,128)} %copy.110) | copy-start | bytes 6291460
  134.7 140.7 %copy-start.1 = (f32[32,16384]{1,0:T(8,128)S(1)}, f32[32,16384]{1,0:T(8,128)}, u32[]{:S(2)}) copy-start(f32[32,16384]{1,0:T(8,128)} %param.13) | copy-start | bytes 6291460
  134.7 140.7 %copy-start.28 = (f32[32,16384]{1,0:T(8,128)S(1)}, f32[32,16384]{1,0:T(8,128)}, u32[]{:S(2)}) copy-start(f32[32,16384]{1,0:T(8,128)} %param.11) | copy-start | bytes 6291460
  134.7 47.2 %collective-permute-start = (f32[32,16384]{1,0:T(8,128)S(1)}, f32[32,16384]{1,0:T(8,128)S(1)}, u32[]{:S(2)}, u32[]{:S(2)}) collective-permute-start(f32[32,16384]{1,0:T(8,128)S(1)} %bitcast.340), channel_id=1, source_target_pairs={{0,1},{1,0},{2,3},{3,2},{4,5},{5,4},{6,7},{7,6},{8,9},{9,8},{10,11... | collective-permute-start | bytes 6291464 | tf_op jit(solution)/shard_map/ppermute | solution.py:78
  183.3 92.1 %collective-permute-start.1 = (f32[32,16384]{1,0:T(8,128)S(1)}, f32[32,16384]{1,0:T(8,128)S(1)}, u32[]{:S(2)}, u32[]{:S(2)}) collective-permute-start(f32[32,16384]{1,0:T(8,128)S(1)} %fusion.149), channel_id=1, source_target_pairs={{0,2},{1,3},{2,0},{3,1},{4,6},{5,7},{6,4},{7,5},{8,10},{9,11},{10,... | collective-permute-start | bytes 6291464 | tf_op jit(solution)/shard_map/ppermute | solution.py:78
  275.8 1.3 copy-start.5
  279.7 9.9 copy-start.11
  365.6 1.3 copy-start.12
  391.9 49.8 %copy-start.19 = (f32[32,128,128]{2,1,0:T(8,128)S(1)}, f32[32,128,128]{2,1,0:T(8,128)}, u32[]{:S(2)}) copy-start(f32[32,128,128]{2,1,0:T(8,128)} %copy.118) | copy-start | bytes 6291460
  394.9 140.0 %copy-start.2 = (f32[32,16384]{1,0:T(8,128)S(1)}, f32[32,16384]{1,0:T(8,128)}, u32[]{:S(2)}) copy-start(f32[32,16384]{1,0:T(8,128)} %param.13) | copy-start | bytes 6291460
  394.9 140.0 %copy-start.6 = (f32[32,16384]{1,0:T(8,128)S(1)}, f32[32,16384]{1,0:T(8,128)}, u32[]{:S(2)}) copy-start(f32[32,16384]{1,0:T(8,128)} %copy-done.5) | copy-start | bytes 6291460
  394.9 46.9 %collective-permute-start.2 = (f32[32,16384]{1,0:T(8,128)S(1)}, f32[32,16384]{1,0:T(8,128)S(1)}, u32[]{:S(2)}, u32[]{:S(2)}) collective-permute-start(f32[32,16384]{1,0:T(8,128)S(1)} %bitcast.341), channel_id=1, source_target_pairs={{0,1},{1,0},{2,3},{3,2},{4,5},{5,4},{6,7},{7,6},{8,9},{9,8},{10,11... | collective-permute-start | bytes 6291464 | tf_op jit(solution)/shard_map/ppermute | solution.py:78
  443.0 92.3 %copy-start.14 = (f32[32,16384]{1,0:T(8,128)}, f32[32,16384]{1,0:T(8,128)S(1)}, u32[]{:S(2)}) copy-start(f32[32,16384]{1,0:T(8,128)S(1)} %fusion.150) | copy-start | bytes 6291460
  443.0 91.8 %collective-permute-start.3 = (f32[32,16384]{1,0:T(8,128)S(1)}, f32[32,16384]{1,0:T(8,128)S(1)}, u32[]{:S(2)}, u32[]{:S(2)}) collective-permute-start(f32[32,16384]{1,0:T(8,128)S(1)} %fusion.150), channel_id=1, source_target_pairs={{0,2},{1,3},{2,0},{3,1},{4,6},{5,7},{6,4},{7,5},{8,10},{9,11},{10,... | collective-permute-start | bytes 6291464 | tf_op jit(solution)/shard_map/ppermute | solution.py:78
  534.9 1.3 copy-start.26
  539.1 9.9 copy-start.13
  624.9 1.3 copy-start.8
  650.9 49.9 %copy-start.20 = (f32[32,128,128]{2,1,0:T(8,128)S(1)}, f32[32,128,128]{2,1,0:T(8,128)}, u32[]{:S(2)}) copy-start(f32[32,128,128]{2,1,0:T(8,128)} %copy.126) | copy-start | bytes 6291460
  650.9 143.0 %copy-start.27 = (f32[32,16384]{1,0:T(8,128)S(1)}, f32[32,16384]{1,0:T(8,128)}, u32[]{:S(2)}) copy-start(f32[32,16384]{1,0:T(8,128)} %copy-done.26) | copy-start | bytes 6291460
  653.9 140.1 %copy-start.3 = (f32[32,16384]{1,0:T(8,128)S(1)}, f32[32,16384]{1,0:T(8,128)}, u32[]{:S(2)}) copy-start(f32[32,16384]{1,0:T(8,128)} %param.13) | copy-start | bytes 6291460
  653.9 140.1 %copy-start.7 = (f32[32,16384]{1,0:T(8,128)S(1)}, f32[32,16384]{1,0:T(8,128)}, u32[]{:S(2)}) copy-start(f32[32,16384]{1,0:T(8,128)} %copy-done.5) | copy-start | bytes 6291460
  653.9 140.0 %copy-start.15 = (f32[32,16384]{1,0:T(8,128)S(1)}, f32[32,16384]{1,0:T(8,128)}, u32[]{:S(2)}) copy-start(f32[32,16384]{1,0:T(8,128)} %copy-done.14) | copy-start | bytes 6291460
  653.9 46.9 %collective-permute-start.4 = (f32[32,16384]{1,0:T(8,128)S(1)}, f32[32,16384]{1,0:T(8,128)S(1)}, u32[]{:S(2)}, u32[]{:S(2)}) collective-permute-start(f32[32,16384]{1,0:T(8,128)S(1)} %bitcast.342), channel_id=1, source_target_pairs={{0,1},{1,0},{2,3},{3,2},{4,5},{5,4},{6,7},{7,6},{8,9},{9,8},{10,11... | collective-permute-start | bytes 6291464 | tf_op jit(solution)/shard_map/ppermute | solution.py:78
  702.1 91.8 %collective-permute-start.5 = (f32[32,16384]{1,0:T(8,128)S(1)}, f32[32,16384]{1,0:T(8,128)S(1)}, u32[]{:S(2)}, u32[]{:S(2)}) collective-permute-start(f32[32,16384]{1,0:T(8,128)S(1)} %fusion.151), channel_id=1, source_target_pairs={{0,2},{1,3},{2,0},{3,1},{4,6},{5,7},{6,4},{7,5},{8,10},{9,11},{10,... | collective-permute-start | bytes 6291464 | tf_op jit(solution)/shard_map/ppermute | solution.py:78
  794.5 1.4 copy-start.16
  798.4 9.9 copy-start.9
  884.1 1.3 copy-start.22
  910.9 49.8 %copy-start.21 = (f32[32,128,128]{2,1,0:T(8,128)S(1)}, f32[32,128,128]{2,1,0:T(8,128)}, u32[]{:S(2)}) copy-start(f32[32,128,128]{2,1,0:T(8,128)} %copy.135) | copy-start | bytes 6291460
  913.8 50.4 %copy-start.23 = (f32[256,16,128]{2,1,0:T(8,128)S(1)}, f32[256,16,128]{2,1,0:T(8,128)}, u32[]{:S(2)}) copy-start(f32[256,16,128]{2,1,0:T(8,128)} %copy-done.22) | copy-start | bytes 6291460
  913.9 46.9 %collective-permute-start.6 = (f32[32,16384]{1,0:T(8,128)S(1)}, f32[32,16384]{1,0:T(8,128)S(1)}, u32[]{:S(2)}, u32[]{:S(2)}) collective-permute-start(f32[32,16384]{1,0:T(8,128)S(1)} %bitcast.343), channel_id=1, source_target_pairs={{0,1},{1,0},{2,3},{3,2},{4,5},{5,4},{6,7},{7,6},{8,9},{9,8},{10,11... | collective-permute-start | bytes 6291464 | tf_op jit(solution)/shard_map/ppermute | solution.py:78
  962.0 91.8 %collective-permute-start.7 = (f32[32,16384]{1,0:T(8,128)S(1)}, f32[32,16384]{1,0:T(8,128)S(1)}, u32[]{:S(2)}, u32[]{:S(2)}) collective-permute-start(f32[32,16384]{1,0:T(8,128)S(1)} %fusion.152), channel_id=1, source_target_pairs={{0,2},{1,3},{2,0},{3,1},{4,6},{5,7},{6,4},{7,5},{8,10},{9,11},{10,... | collective-permute-start | bytes 6291464 | tf_op jit(solution)/shard_map/ppermute | solution.py:78
  964.5 89.3 %copy-start.4 = (f32[32,16384]{1,0:T(8,128)S(1)}, f32[32,16384]{1,0:T(8,128)}, u32[]{:S(2)}) copy-start(f32[32,16384]{1,0:T(8,128)} %param.13) | copy-start | bytes 6291460
  964.5 89.3 %copy-start.17 = (f32[32,16384]{1,0:T(8,128)S(1)}, f32[32,16384]{1,0:T(8,128)}, u32[]{:S(2)}) copy-start(f32[32,16384]{1,0:T(8,128)} %copy-done.16) | copy-start | bytes 6291460
